TPU v7x, 32 devices: a whole 2x2x4 slice. The times are simulated.
32 devices in a mesh: row: 4 (over y, x), col: 8 (over z, core).
Axes of the slice: x: 2, y: 2, z: 4, core: 2. Of those that a mesh axis runs over, the one named last changes fastest.
Arguments:
- features: bfloat16 [32768, 128], P(('row', 'col')), may hold values from -24 to 24
- tile_rows: int32 [4, 8, 1024], P('row', 'col'), may hold values from 0 to 63
- tile_cols: int32 [4, 8, 1024], P('row', 'col'), may hold values from 0 to 31
- edge_lists: int32 [2, 4, 8, 1024, 128], P(None, 'row', 'col'), may hold values from -16 to 127
- tile_counts: int32 [4, 8], P('row', 'col'), may hold values from 128 to 1024, as said below
Outputs:
- hop_one: bfloat16 [32768, 128], P(('row', 'col'))
- hop_two: bfloat16 [32768, 128], P(('row', 'col'))
Inputs may be any that keep to these rules, and one draw needn't show every extreme that they name: `tile_counts`: live tile slots of a block; some block has exactly 1024. `edge_lists`: a negative entry marks an empty edge slot; slots at or past a block's count hold arbitrary entries. `tile_rows`: a tile may occur in several slots; slots at or past a block's count hold arbitrary entries. `tile_cols`: slots at or past a block's count hold arbitrary entries.
All inputs are finite; a program needn't handle non-finite values.
Results may differ from a plain program's by a relative error of at most 0.0058.
Values may be sent and summed in bfloat16 or wider, within the bound.
A program may use at most 192 MiB of HBM per device.

v0:
```python
import functools

import jax
import jax.numpy as jnp
from jax import lax
from jax.experimental import pallas as pl
from jax.experimental.pallas import tpu as pltpu
from jax.sharding import PartitionSpec as P

TILE = 128
ROWS_MIN = 16
BUILD_UNROLL = 32
BUILD_SLOTS = 6
APPLY_UNROLL = 64
APPLY_SLOTS = 4
HOT = jnp.float8_e4m3fn
HOT_ROWS = 32
EXTRA = 16
SLOT_BITS = 11
CODE_BITS = 8
PIECES = 4
RELAY_LAG = 3
EARLY = 1
CORES = 2
MESH_ID = pl.DeviceIdType.MESH
VMEM_SPEC = pl.BlockSpec(memory_space=pltpu.VMEM)
SMEM_SPEC = pl.BlockSpec(memory_space=pltpu.SMEM)
ANY_SPEC = pl.BlockSpec(memory_space=pl.ANY)
HBM_SPEC = pl.BlockSpec(memory_space=pltpu.HBM)


def place_of():
    row, col = lax.axis_index("row"), lax.axis_index("col")
    return row, col, lax.rem(col, CORES), col // CORES


def order_kernel(
    own, n_chip, pairs, count_ref, rows_hbm, cols_hbm, features_hbm,
    order_ref, turned_ref, rows_ref, cols_ref, features_ref, sem
):
    loads = [
        pltpu.make_async_copy(source, target, sem.at[i])
        for i, (source, target) in enumerate(
            (
                (rows_hbm, rows_ref),
                (cols_hbm, cols_ref),
                (features_hbm, features_ref),
            )
        )
    ]
    for load in loads:
        load.start()
    slots = rows_ref.shape[-1]
    bins = CORES * n_chip * own
    bf16, f32 = jnp.bfloat16, jnp.float32
    _, _, core, chip = place_of()

    def iota(shape, dim):
        return lax.broadcasted_iota(jnp.int32, shape, dim)

    def hot(mask):
        return jnp.where(mask, 1.0, 0.0).astype(bf16)

    def mul(x, y):
        return jnp.dot(x.astype(bf16), y.astype(bf16), preferred_element_type=f32)

    loads[0].wait()
    loads[1].wait()
    slot = iota((1, slots), 1)
    alive = slot < count_ref[0]
    rows = jnp.where(alive, rows_ref[...], 0)
    cols = jnp.where(alive, cols_ref[...], 0)
    owner = rows // own
    target = owner // CORES
    other = jnp.where(lax.rem(owner, CORES) == core, 0, 1)
    rank = jnp.where(chip < n_chip // 2, n_chip - 1 - target, target)
    local = rank * own + lax.rem(rows, own)
    bin_of = jnp.where(alive, other * n_chip * own + local, -1)
    belongs = bin_of == iota((bins, slots), 0)
    ranks = mul(hot(belongs), hot(iota((slots, slots), 0) <= iota((slots, slots), 1)))
    totals = jnp.broadcast_to(ranks[:, slots - 1 :], (bins, TILE)).astype(jnp.int32)
    halves = (totals + 1) // 2
    before = hot(iota((bins, bins), 1) < iota((bins, bins), 0))
    offsets = 32.0 * mul(before, (halves // 32).astype(f32)) + mul(before, (halves % 32).astype(f32))
    spots = jnp.where(belongs, ranks - 1.0 + 2.0 * offsets[:, :1], 0.0)
    spot = jnp.where(alive, jnp.sum(spots, axis=0, keepdims=True), -1.0)
    odd = jnp.where(alive, spot.astype(jnp.int32) % 2, -1)
    facts = []
    for side in range(2):
        here = odd == side
        facts += [
            jnp.where(here, fact, 0)
            for fact in (slot // 32, slot % 32, jnp.where(here, 1, 0), cols, local)
        ]
    facts = jnp.concatenate(
        [fact.astype(f32) for fact in facts] + [jnp.zeros((EXTRA - len(facts), slots), f32)], axis=0
    )
    pair_of = jnp.broadcast_to(spot, (TILE, slots)).T.astype(jnp.int32) >> 1
    for start in range(0, pairs, TILE):
        found = mul(facts, hot(pair_of == iota((slots, TILE), 1) + start)).astype(jnp.int32)
        places = [32 * found[i : i + 1] + found[i + 1 : i + 2] + found[i + 2 : i + 3] for i in (0, 5)]
        row, cols = found[4:5], (found[3:4], found[8:9])
        order_ref[:, start : start + TILE] = (row << (2 * SLOT_BITS)) + (places[1] << SLOT_BITS) + places[0]
        order_ref[:, pairs + start : pairs + start + TILE] = (
            (cols[1] << (2 * CODE_BITS)) + (cols[0] << CODE_BITS) + row
        )
    end = jnp.sum(halves.astype(f32), axis=0, keepdims=True).astype(jnp.int32)
    order_ref[:, 2 * pairs : 2 * pairs + bins] = offsets.T[0:1, :].astype(jnp.int32)
    order_ref[:, 2 * pairs + bins : 2 * pairs + bins + TILE] = end
    loads[2].wait()
    for tile in range(own):
        block = features_ref[tile * TILE : (tile + 1) * TILE, :].astype(f32).T
        turned_ref[tile] = block.astype(bf16)


def spans_of(order_ref, pairs, half_bins, other, first, last):
    base = 2 * pairs + other * half_bins
    return order_ref[0, base], order_ref[0, base + first], order_ref[0, base + last]


def build_kernel(half_bins, other, order_ref, edges_ref, *refs):
    *previous, store_ref, degree_ref, made, degree_acc, sem = refs
    degree_acc[...] = jnp.zeros_like(degree_acc)
    _, low, high = spans_of(order_ref, store_ref.shape[0], half_bins, other, 0, half_bins)
    pairs = BUILD_UNROLL // 2
    turns = (high - low + pairs - 1) // pairs
    mask = 2**SLOT_BITS - 1
    cells = [
        (lax.broadcasted_iota(jnp.int32, (HOT_ROWS, TILE), 0) + start).astype(jnp.int8)
        for start in range(0, TILE, HOT_ROWS)
    ]

    def hot(ids):
        ids = jnp.broadcast_to(ids, (HOT_ROWS, TILE)).astype(jnp.int8)
        return jnp.concatenate(
            [jnp.where(ids == cell, HOT(1), HOT(0)) for cell in cells], axis=0
        )

    def out_copy(turn):
        side = lax.rem(turn, BUILD_SLOTS)
        return pltpu.make_async_copy(
            made.at[side], store_ref.at[pl.ds(turn * pairs, pairs)], sem.at[side]
        )

    def visit(turn, carry):
        side = lax.rem(turn, BUILD_SLOTS)

        @pl.when(turn >= BUILD_SLOTS)
        def _():
            out_copy(turn - BUILD_SLOTS).wait()

        for pair in range(pairs):
            counts = []
            base = low + turn * pairs + pair
            code = order_ref[0, base]
            live = jnp.where(base < high, code, 0)
            for half in range(2):
                slot = ((live >> (half * SLOT_BITS)) & mask) - 1
                safe = jnp.maximum(slot, 0)
                dst = jnp.where(slot >= 0, edges_ref[0, pl.ds(safe, 1), :], -1)
                src = edges_ref[1, pl.ds(safe, 1), :]
                both = lax.dot_general(
                    hot(src), hot(dst), (((1,), (1,)), ((), ())), preferred_element_type=jnp.float32
                )
                made[side, pair, half * TILE : (half + 1) * TILE] = both.astype(jnp.bfloat16)
                counts.append(jnp.sum(both.reshape(TILE // 8, 8, TILE), axis=0))
            degree_acc[live >> (2 * SLOT_BITS)] += counts[0] + counts[1]
        out_copy(turn).start()
        return carry

    lax.fori_loop(0, turns, visit, 0)

    for back in range(BUILD_SLOTS, 0, -1):

        @pl.when(turns >= back)
        def _():
            out_copy(turns - back).wait()

    degree = jnp.sum(degree_acc[...], axis=1)
    degree_ref[...] = degree + previous[0][...] if previous else degree


def apply_kernel(half_bins, first_row, orders, stores, source_ref, out_ref, held, acc, sem):
    rows = out_ref.shape[0]
    pairs = APPLY_UNROLL // 2
    total_pairs = stores[0].shape[0]
    lists, spans, turns = [], [], []
    for other, order_ref in enumerate(orders):
        start, low, high = spans_of(
            order_ref, total_pairs, half_bins, other, first_row, first_row + rows
        )
        lists.append(start)
        spans.append((low, high))
        turns.append((high - low + pairs - 1) // pairs)
    code_mask = 2**CODE_BITS - 1

    def fetch(turn):
        slot = lax.rem(turn, APPLY_SLOTS)
        for other in range(2):
            local = turn - other * turns[0]

            @pl.when((local >= 0) & (local < turns[other]))
            def _():
                start = spans[other][0] - lists[other] + local * pairs
                pltpu.make_async_copy(
                    stores[other].at[pl.ds(start, pairs)], held.at[slot], sem.at[slot]
                ).start()

    for turn in range(APPLY_SLOTS - 1):
        fetch(turn)
    acc[...] = jnp.zeros_like(acc)

    for other in range(2):
        order_ref = orders[other]
        low, high = spans[other]
        offset = other * source_ref.shape[0] // 2

        def visit(turn, carry):
            slot = lax.rem(turn, APPLY_SLOTS)
            pltpu.make_async_copy(
                stores[0].at[pl.ds(0, pairs)], held.at[slot], sem.at[slot]
            ).wait()
            fetch(turn + APPLY_SLOTS - 1)
            for pair in range(pairs):
                base = low + (turn - other * turns[0]) * pairs + pair
                code = order_ref[0, total_pairs + base]
                left = (code >> CODE_BITS) & code_mask
                right = code >> (2 * CODE_BITS)
                sources = jnp.concatenate(
                    [source_ref[offset + left], source_ref[offset + right]], axis=1
                )
                place = jnp.where(base < high, (code & code_mask) - first_row, rows)
                acc[place] += jnp.dot(
                    sources, held[slot, pair], preferred_element_type=jnp.float32
                )
            return carry

        lax.fori_loop(other * turns[0], turns[0] + other * turns[1], visit, 0)
    out_ref[...] = acc[:rows].astype(jnp.bfloat16)


def greet(targets):
    barrier = pltpu.get_barrier_semaphore()
    for target in targets:
        pl.semaphore_signal(barrier, inc=1, device_id=target, device_id_type=MESH_ID)
    pl.semaphore_wait(barrier, len(targets))


def row_peers(n_row, side=0):
    row, col, core, chip = place_of()
    if side:
        col = chip * CORES + 1 - core
    return [(lax.rem(row + d, n_row), col) for d in range(1, n_row)]


def sibling_peers(n_col):
    row, col, _, _ = place_of()
    return [(row, lax.rem(col + CORES * d, n_col)) for d in range(1, n_col // CORES)]


def partner_of():
    row, col, core, chip = place_of()
    return (row, chip * CORES + 1 - core)


def remote(src, dst, send_sem, recv_sem, target):
    return pltpu.make_async_remote_copy(
        src_ref=src,
        dst_ref=dst,
        send_sem=send_sem,
        recv_sem=recv_sem,
        device_id=target,
        device_id_type=MESH_ID,
    )


def send(*args):
    copy = remote(*args)
    copy.start()
    return copy


def start_kernel(n_row, n_col, part, *refs):
    blocks = refs[:n_row]
    gathered_ref, root_ref, taken, theirs, roots = refs[n_row : n_row + 5]
    deg_send, deg_recv, near_send, near_recv, root_send, root_recv = refs[n_row + 5 :]
    row, col, core, chip = place_of()
    n_chip = n_col // CORES
    own = root_ref.shape[0]
    partner = partner_of()
    siblings = sibling_peers(n_col)
    mine, cross = row_peers(n_row), row_peers(n_row, 1)
    greet(siblings + mine + cross + [partner])
    copies = []
    low_half = chip < n_chip // 2
    for d, target in enumerate(siblings):
        rank = target[1] // CORES
        start = jnp.where(low_half, n_chip - 1 - rank, rank) * own
        copies.append(
            send(
                part.at[pl.ds(pl.multiple_of(start, own), own)],
                taken.at[d],
                deg_send.at[d],
                deg_recv.at[d],
                target,
            )
        )
    near = []
    for d in range(n_row):
        near.append(send(blocks[d], theirs.at[d], near_send.at[d], near_recv.at[d], partner))
    mine_rank = jnp.where(low_half, n_chip - 1 - chip, chip)
    degree = part[pl.ds(pl.multiple_of(mine_rank * own, own), own), :]
    for d, copy in enumerate(copies):
        copy.wait_recv()
        degree = degree + taken[d]
    root = lax.rsqrt(1.0 + degree)
    root_ref[...] = root
    roots[0, 0] = root
    root_copies = []
    for side, targets in ((0, mine), (1, [partner] + cross)):
        for d, target in enumerate(targets):
            d += 1 - side
            root_copies.append(
                send(roots.at[0, 0], roots.at[side, d], root_send.at[side, d], root_recv.at[side, d], target)
            )

    def scale(side, d, source, root):
        start = side * n_row * own + lax.rem(row + n_row - d, n_row) * own
        for tile in range(own):
            gathered_ref[start + tile] = (
                source[tile].astype(jnp.float32) * root[tile : tile + 1, :]
            ).astype(jnp.bfloat16)

    scale(0, 0, blocks[0], root)
    for copy in root_copies:
        copy.wait_recv()
    for d in range(1, n_row):
        scale(0, d, blocks[d], roots[0, d])
    for d in range(n_row):
        near[d].wait_recv()
        scale(1, d, theirs.at[d], roots[1, d])
    for copy in copies + near + root_copies:
        copy.wait_send()


def sum_kernel(n_row, n_col, spread, *refs):
    parts, given, refs = refs[: EARLY + 1], refs[EARLY + 1 : 2 * EARLY + 1], refs[2 * EARLY + 1 :]
    if spread:
        root_ref, hop_ref, gathered_ref, comes, goes, *sems = refs
        send_sem, recv_sem, row_send, row_recv, near_send, near_recv = sems
    else:
        root_ref, hop_ref, comes, goes, send_sem, recv_sem = refs
    row, col, core, chip = place_of()
    n_chip = n_col // CORES
    own = root_ref.shape[0]
    size = own // PIECES
    partner = partner_of()
    up = (row, lax.rem(col + CORES, n_col))
    down = (row, lax.rem(col + n_col - CORES, n_col))
    mine = row_peers(n_row)
    greet([up, down] + ([partner] + mine if spread else []))
    last = n_chip - 1
    low_half = chip < n_chip // 2
    early = jnp.where(low_half, 0, 1)
    depth = jnp.where(low_half, chip, last - chip)

    def block(rank, piece):
        if rank < EARLY:
            return parts[rank].at[piece * size : (piece + 1) * size]
        start = (rank - EARLY) * own + piece * size
        return parts[EARLY].at[start : start + size]

    def hop_copy(way, k, piece, source=None):
        return remote(
            goes.at[way, k, piece] if source is None else source,
            comes.at[way, k, piece],
            send_sem.at[way, k, piece],
            recv_sem.at[way, k, piece],
            (row, lax.rem(col + jnp.where(way == 0, CORES, n_col - CORES), n_col)),
        )

    flow = [(k, piece) for piece in range(PIECES) for k in range(last)]
    timed = [(i, 0, *f) for i, f in enumerate(flow)]
    timed += [(i + RELAY_LAG, 1, *f) for i, f in enumerate(flow) if f[0] < n_chip // 2 - 1]

    def steps():
        for _, late, k, piece in sorted(timed):
            way = 1 - early if late else early
            ahead = k < (depth if late else last - depth)
            yield k, piece, late, way, ahead

    for k, piece, late, way, ahead in steps():
        source = block(last - k if late else k, piece)

        def relay(arrived):
            goes[way, k, piece] = (
                source[...].astype(jnp.float32) + arrived.astype(jnp.float32)
            ).astype(jnp.bfloat16)
            hop_copy(way, k, piece).start()

        def relay_waited():
            hop_copy(way, k, piece).wait_recv()
            relay(comes[way, k, piece])

        if late:
            pl.when(ahead)(relay_waited)
        elif k >= EARLY:
            pl.when(ahead & (depth == 0))(lambda: hop_copy(way, k, piece, source).start())
            pl.when(ahead & (depth > 0))(relay_waited)
        else:
            pl.when(ahead & (depth == 1))(
                lambda: relay(given[k][piece * size : (piece + 1) * size])
            )
            pl.when(ahead & (depth > 1))(relay_waited)

    row_copies, near_copies = {}, {}
    for piece in range(PIECES):
        early_k = jnp.minimum(last - depth, last - 1)

        @pl.when(depth > 0)
        def _():
            hop_copy(early, early_k, piece).wait_recv()

        hop_copy(1 - early, depth, piece).wait_recv()
        start = pl.multiple_of((last - depth - EARLY) * own, own) + piece * size
        total = parts[EARLY][pl.ds(start, size)].astype(jnp.float32)
        near = comes[early, early_k, piece].astype(jnp.float32)
        total = total + jnp.where(depth > 0, near, 0.0)
        total = total + comes[1 - early, depth, piece].astype(jnp.float32)
        roots = [root_ref[piece * size + tile : piece * size + tile + 1, :] for tile in range(size)]
        if spread:
            start = row * own + piece * size
            for tile in range(size):
                gathered_ref[start + tile] = (total[tile] * (roots[tile] * roots[tile])).astype(
                    jnp.bfloat16
                )
            for d, target in enumerate(mine):
                place = gathered_ref.at[pl.ds(start, size)]
                row_copies[piece, d] = send(
                    place, place, row_send.at[piece, d], row_recv.at[piece, d], target
                )
            near_copies[piece, 0] = send(
                gathered_ref.at[pl.ds(start, size)],
                gathered_ref.at[pl.ds(n_row * own + start, size)],
                near_send.at[piece, 0],
                near_recv.at[piece, 0],
                partner,
            )
        for tile in range(size):
            place = (piece * size + tile) * TILE
            hop_ref[place : place + TILE, :] = (total[tile] * roots[tile]).T.astype(jnp.bfloat16)
    for (piece, d), copy in row_copies.items():
        copy.wait_recv()
        start = lax.rem(row + n_row - d - 1, n_row) * own + piece * size
        near_copies[piece, d + 1] = send(
            gathered_ref.at[pl.ds(start, size)],
            gathered_ref.at[pl.ds(n_row * own + start, size)],
            near_send.at[piece, d + 1],
            near_recv.at[piece, d + 1],
            partner,
        )
    for copy in near_copies.values():
        copy.wait_recv()
    for copy in list(row_copies.values()) + list(near_copies.values()):
        copy.wait_send()
    for k, piece, late, way, ahead in steps():
        if not late and k < EARLY:
            ahead = ahead & (depth > 0)
        pl.when(ahead)(lambda: hop_copy(way, k, piece).wait_send())


def sems(*shape):
    return pltpu.SemaphoreType.DMA(shape)


def comm_params(ident):
    return pltpu.CompilerParams(
        collective_id=ident, has_side_effects=True, vmem_limit_bytes=48 * 2**20
    )


def full_params():
    return pltpu.CompilerParams(vmem_limit_bytes=67043328)


def build_params():
    return pltpu.CompilerParams(vmem_limit_bytes=65 * 10**6)


def plain_params():
    return pltpu.CompilerParams(vmem_limit_bytes=48 * 2**20)


def local(features, tile_rows, tile_cols, edge_lists, tile_counts):
    node_count, feat_width = features.shape
    n_row, n_col = lax.axis_size("row"), lax.axis_size("col")
    n_chip = n_col // CORES
    own = node_count // TILE
    half_tiles = own * n_chip
    source_tiles = own * n_row
    slots = tile_rows.shape[-1]
    bf16, f32 = jnp.bfloat16, jnp.float32
    spare = max(BUILD_UNROLL, APPLY_UNROLL)
    pairs = -(-(slots + CORES * half_tiles + spare) // (2 * TILE)) * TILE
    swap = [(i, i + 1 - 2 * (i % CORES)) for i in range(n_col)]
    edges = edge_lists.reshape(2, slots, TILE)

    edges_b = lax.ppermute(edges, "col", swap)
    codes = 2 * pairs + -(-(CORES * half_tiles) // TILE) * TILE + TILE
    order, turned = pl.pallas_call(
        functools.partial(order_kernel, own, n_chip, pairs),
        out_shape=[
            jax.ShapeDtypeStruct((1, codes), jnp.int32),
            jax.ShapeDtypeStruct((own, feat_width, TILE), bf16),
        ],
        in_specs=[SMEM_SPEC] + [HBM_SPEC] * 3,
        out_specs=[VMEM_SPEC] * 2,
        scratch_shapes=[
            pltpu.VMEM((1, slots), jnp.int32),
            pltpu.VMEM((1, slots), jnp.int32),
            pltpu.VMEM((node_count, feat_width), bf16),
            sems(3),
        ],
        compiler_params=full_params(),
        name="order",
    )(tile_counts[0], tile_rows[0], tile_cols[0], features)
    blocks = [turned] + [
        lax.ppermute(turned, "row", [(i, (i + d) % n_row) for i in range(n_row)])
        for d in range(1, n_row)
    ]
    order_b = lax.ppermute(order, "col", swap)

    def build(order, edges, *previous):
        return pl.pallas_call(
            functools.partial(build_kernel, half_tiles, len(previous)),
            in_specs=[SMEM_SPEC, VMEM_SPEC] + [VMEM_SPEC] * len(previous),
            out_specs=[ANY_SPEC, VMEM_SPEC],
            scratch_shapes=[
                pltpu.VMEM((BUILD_SLOTS, BUILD_UNROLL // 2, 2 * TILE, TILE), bf16),
                pltpu.VMEM((half_tiles, 8, TILE), f32),
                sems(BUILD_SLOTS),
            ],
            out_shape=[
                jax.ShapeDtypeStruct((pairs, 2 * TILE, TILE), bf16),
                jax.ShapeDtypeStruct((half_tiles, TILE), f32),
            ],
            compiler_params=build_params(),
            cost_estimate=pl.CostEstimate(flops=10**10, bytes_accessed=0, transcendentals=0),
            name="build",
        )(order, edges, *previous)

    store_a, degree_a = build(order, edges)
    store_b, degree = build(order_b, edges_b, degree_a)

    gathered_type = jax.ShapeDtypeStruct((CORES * source_tiles, feat_width, TILE), bf16)
    gathered, root = pl.pallas_call(
        functools.partial(start_kernel, n_row, n_col),
        out_shape=[gathered_type, jax.ShapeDtypeStruct((own, TILE), f32)],
        in_specs=[VMEM_SPEC] * (1 + n_row),
        out_specs=[VMEM_SPEC] * 2,
        scratch_shapes=[
            pltpu.VMEM((n_chip - 1, own, TILE), f32),
            pltpu.VMEM((n_row, own, feat_width, TILE), bf16),
            pltpu.VMEM((2, n_row, own, TILE), f32),
            sems(n_chip - 1),
            sems(n_chip - 1),
            sems(n_row),
            sems(n_row),
            sems(2, n_row),
            sems(2, n_row),
        ],
        compiler_params=comm_params(0),
        name="start",
    )(degree, *blocks)

    def apply(sources, ranks, after):
        rows = len(ranks) * own

        def body(order_a, order_b, store_a, store_b, sources, after, *refs):
            apply_kernel(
                half_tiles, ranks[0] * own, (order_a, order_b), (store_a, store_b), sources, *refs
            )

        return pl.pallas_call(
            body,
            in_specs=[SMEM_SPEC] * 2 + [ANY_SPEC] * 2 + [VMEM_SPEC, ANY_SPEC],
            out_specs=VMEM_SPEC,
            scratch_shapes=[
                pltpu.VMEM((APPLY_SLOTS, APPLY_UNROLL // 2, 2 * TILE, TILE), bf16),
                pltpu.VMEM((rows + 1, feat_width, TILE), f32),
                sems(APPLY_SLOTS),
            ],
            out_shape=jax.ShapeDtypeStruct((rows, feat_width, TILE), bf16),
            compiler_params=plain_params(),
            cost_estimate=pl.CostEstimate(flops=10**10, bytes_accessed=0, transcendentals=0),
            name="apply",
        )(order, order_b, store_a, store_b, sources, after)

    ends = [
        (a * CORES + core, b * CORES + core)
        for a, b in ((0, 1), (n_chip - 1, n_chip - 2))
        for core in range(CORES)
    ]

    def apply_all(sources):
        parts, given, after = [], [], sources
        for rank in range(EARLY):
            parts.append(apply(sources, [rank], after))
            given.append(lax.ppermute(parts[-1], "col", ends))
            after = parts[-1]
        parts.append(apply(sources, list(range(EARLY, n_chip)), after))
        return parts + given

    def collect(parts, spread):
        size = own // PIECES
        outs = [jax.ShapeDtypeStruct((node_count, feat_width), bf16)]
        semaphores = [sems(2, n_chip - 1, PIECES)] * 2
        if spread:
            outs.append(gathered_type)
            semaphores += [sems(PIECES, n_row - 1)] * 2 + [sems(PIECES, n_row)] * 2
        return pl.pallas_call(
            functools.partial(sum_kernel, n_row, n_col, spread),
            out_shape=outs,
            in_specs=[VMEM_SPEC] * (len(parts) + 1),
            out_specs=[VMEM_SPEC] * len(outs),
            scratch_shapes=[pltpu.VMEM((2, n_chip - 1, PIECES, size, feat_width, TILE), bf16)] * 2
            + semaphores,
            compiler_params=comm_params(1 if spread else 2),
            name="spread" if spread else "finish",
        )(*parts, root)

    hop_one, gathered = collect(apply_all(gathered), True)
    (hop_two,) = collect(apply_all(gathered), False)
    return (hop_one, hop_two)


def solution(mesh):
    placed = (
        P(("row", "col"), None),
        P("row", "col", None),
        P("row", "col", None),
        P(None, "row", "col", None, None),
        P("row", "col"),
    )
    return jax.shard_map(
        local,
        mesh=mesh,
        in_specs=placed,
        out_specs=(P(("row", "col"), None), P(("row", "col"), None)),
        check_vma=False,
    )
```

profile of v0, /device:TPU:0, one launch (start us, length us, event | category | flops | bytes accessed | tf_op | source)
XLA Modules:
  0.0 115.2 jit_solution(7834519121302600628)
XLA Ops:
  0.6 0.6 collective-permute-start.1
  1.8 2.8 %order.1 = (s32[1,1536]{1,0:T(1,128)}, bf16[8,128,128]{2,1,0:T(8,128)(2,1)}) custom-call(s32[1]{0:T(128)} %bitcast.4.count_ref, s32[1,1024]{1,0:T(1,128)} %bitcast.5, s32[1,1024]{1,0:T(1,128)} %bitcast.6, bf16[1024,128]{1,0:T(8,128)(2,1)} %features_hbm.1), custom_call_target="tpu_custom_call" | custom-call | tf_op jit(solution)/shard_map/order/pallas_call | solution.py:510
  4.7 0.0 copy-start
  4.7 0.0 copy-start.1
  4.7 3.5 %collective-permute-start.4 = (bf16[8,128,128]{2,1,0:T(8,128)(2,1)}, bf16[8,128,128]{2,1,0:T(8,128)(2,1)S(1)}, u32[]{:S(2)}, u32[]{:S(2)}) collective-permute-start(bf16[8,128,128]{2,1,0:T(8,128)(2,1)} %get-tuple-element.17.refs_0_), channel_id=1, source_target_pairs={{0,24},{8,0},{16,8},{24,16},{1,25},{9,1},{17,9},{25,17},{2,26},{10... | collective-permute-start | bytes 786440 | tf_op jit(solution)/shard_map/ppermute | solution.py:528
  8.2 0.5 collective-permute-start.3
  8.7 0.6 collective-permute-start.2
  9.3 0.0 collective-permute-start
  9.3 4.2 %build.2 = (bf16[640,256,128]{2,1,0:T(8,128)(2,1)}, f32[32,128]{1,0:T(8,128)}) custom-call(s32[1,1536]{1,0:T(1,128)} %get-tuple-element.12.order_ref.order_a, s32[2,1024,128]{2,1,0:T(8,128)} %bitcast.8), custom_call_target="tpu_custom_call" | custom-call | flops 10000000000 | tf_op jit(solution)/shard_map/build/pallas_call | solution.py:534
  13.5 0.0 collective-permute-done.order_ref.order_b
  13.5 0.0 copy-start.2
  13.5 0.0 collective-permute-done.1.edges_ref
  13.5 0.6 copy-done.2
  14.1 5.0 %build.3 = (bf16[640,256,128]{2,1,0:T(8,128)(2,1)}, f32[32,128]{1,0:T(8,128)}) custom-call(s32[1,1536]{1,0:T(1,128)} %copy-done.2, s32[2,1024,128]{2,1,0:T(8,128)} %collective-permute-done.1.edges_ref, f32[32,128]{1,0:T(8,128)} %get-tuple-element.14.refs_0_), custom_call_target="tpu_custom_call" | custom-call | flops 10000000000 | tf_op jit(solution)/shard_map/build/pallas_call | solution.py:534
  19.1 0.0 collective-permute-done.4.refs_3_
  19.1 3.3 %collective-permute-done.3.refs_2_ = bf16[8,128,128]{2,1,0:T(8,128)(2,1)S(1)} collective-permute-done((bf16[8,128,128]{2,1,0:T(8,128)(2,1)}, bf16[8,128,128]{2,1,0:T(8,128)(2,1)S(1)}, u32[]{:S(2)}, u32[]{:S(2)}) %collective-permute-start.3) | collective-permute-done | bytes 262176 | tf_op jit(solution)/shard_map/ppermute | solution.py:528
  22.5 0.0 collective-permute-done.2.refs_1_
  22.5 0.0 copy-done
  22.5 0.0 copy-start.5
  22.5 0.7 copy-done.5
  23.2 13.3 %start.1 = (bf16[64,128,128]{2,1,0:T(8,128)(2,1)S(1)}, f32[8,128]{1,0:T(8,128)S(1)}) custom-call(f32[32,128]{1,0:T(8,128)S(1)} %copy-done.5, bf16[8,128,128]{2,1,0:T(8,128)(2,1)S(1)} %copy-done, bf16[8,128,128]{2,1,0:T(8,128)(2,1)S(1)} %collective-permute-done.2.refs_1_, bf16[8,128,128]{2,1,0:T(8,128)(2,1)S(1)} %collective-permute-done.3.refs_2_, ...), custom_call_target="tpu_custom_call" | custom-call | tf_op jit(solution)/shard_map/start/pallas_call | solution.py:556
  36.5 0.0 copy-done.1
  36.5 0.0 copy-start.3
  36.5 0.7 copy-done.3
  37.2 3.9 %apply.4.after.refs_0_ = bf16[8,128,128]{2,1,0:T(8,128)(2,1)S(1)} custom-call(s32[1,1536]{1,0:T(1,128)S(1)} %copy-done.1, s32[1,1536]{1,0:T(1,128)S(1)} %copy-done.3, bf16[640,256,128]{2,1,0:T(8,128)(2,1)} %get-tuple-element.13.store_a, bf16[640,256,128]{2,1,0:T(8,128)(2,1)} %get-tuple-element.15.store_b, ...), custom_call_target="tpu_custom_call" | custom-call | flops 10000000000 | tf_op jit(solution)/shard_map/apply/pallas_call | solution.py:584
  41.1 0.0 copy-start.4
  41.1 2.5 %collective-permute-start.5 = (bf16[8,128,128]{2,1,0:T(8,128)(2,1)S(1)}, bf16[8,128,128]{2,1,0:T(8,128)(2,1)S(1)}, u32[]{:S(2)}, u32[]{:S(2)}) collective-permute-start(bf16[8,128,128]{2,1,0:T(8,128)(2,1)S(1)} %apply.4.after.refs_0_), channel_id=1, source_target_pairs={{0,2},{1,3},{6,4},{7,5},{8,10},{9,11},{14,12},{15,13},{16,18},{17,... | collective-permute-start | bytes 786440 | tf_op jit(solution)/shard_map/ppermute | solution.py:609
  43.6 4.7 %apply.5.refs_1_ = bf16[24,128,128]{2,1,0:T(8,128)(2,1)S(1)} custom-call(s32[1,1536]{1,0:T(1,128)S(1)} %copy-done.1, s32[1,1536]{1,0:T(1,128)S(1)} %copy-done.3, bf16[640,256,128]{2,1,0:T(8,128)(2,1)} %get-tuple-element.13.store_a, bf16[640,256,128]{2,1,0:T(8,128)(2,1)} %get-tuple-element.15.store_b, ...), custom_call_target="tpu_custom_call" | custom-call | flops 10000000000 | tf_op jit(solution)/shard_map/apply/pallas_call | solution.py:584
  48.3 1.1 collective-permute-done.5.refs_2_
  49.4 27.4 %spread.1 = (bf16[1024,128]{1,0:T(8,128)(2,1)S(1)}, bf16[64,128,128]{2,1,0:T(8,128)(2,1)S(1)}) custom-call(bf16[8,128,128]{2,1,0:T(8,128)(2,1)S(1)} %apply.4.after.refs_0_, bf16[24,128,128]{2,1,0:T(8,128)(2,1)S(1)} %apply.5.refs_1_, bf16[8,128,128]{2,1,0:T(8,128)(2,1)S(1)} %collective-permute-done.5.refs_2_, f32[8,128]{1,0:T(8,128)S(1)} %get-tuple-element.19.refs_3_), custom_call_target="tpu_custom_call" | custom-call | tf_op jit(solution)/shard_map/spread/pallas_call | solution.py:621
  76.8 0.0 copy-done.4
  76.8 3.9 %apply.6.after.refs_0_ = bf16[8,128,128]{2,1,0:T(8,128)(2,1)S(1)} custom-call(s32[1,1536]{1,0:T(1,128)S(1)} %copy-done.1, s32[1,1536]{1,0:T(1,128)S(1)} %copy-done.4, bf16[640,256,128]{2,1,0:T(8,128)(2,1)} %get-tuple-element.13.store_a, bf16[640,256,128]{2,1,0:T(8,128)(2,1)} %get-tuple-element.15.store_b, ...), custom_call_target="tpu_custom_call" | custom-call | flops 10000000000 | tf_op jit(solution)/shard_map/apply/pallas_call | solution.py:584
  80.8 7.5 %collective-permute-start.6 = (bf16[8,128,128]{2,1,0:T(8,128)(2,1)S(1)}, bf16[8,128,128]{2,1,0:T(8,128)(2,1)S(1)}, u32[]{:S(2)}, u32[]{:S(2)}) collective-permute-start(bf16[8,128,128]{2,1,0:T(8,128)(2,1)S(1)} %apply.6.after.refs_0_), channel_id=1, source_target_pairs={{0,2},{1,3},{6,4},{7,5},{8,10},{9,11},{14,12},{15,13},{16,18},{17,... | collective-permute-start | bytes 786440 | tf_op jit(solution)/shard_map/ppermute | solution.py:609
  88.3 4.7 %apply.7.refs_1_ = bf16[24,128,128]{2,1,0:T(8,128)(2,1)S(1)} custom-call(s32[1,1536]{1,0:T(1,128)S(1)} %copy-done.1, s32[1,1536]{1,0:T(1,128)S(1)} %copy-done.4, bf16[640,256,128]{2,1,0:T(8,128)(2,1)} %get-tuple-element.13.store_a, bf16[640,256,128]{2,1,0:T(8,128)(2,1)} %get-tuple-element.15.store_b, ...), custom_call_target="tpu_custom_call" | custom-call | flops 10000000000 | tf_op jit(solution)/shard_map/apply/pallas_call | solution.py:584
  93.0 1.4 %collective-permute-done.6.refs_2_ = bf16[8,128,128]{2,1,0:T(8,128)(2,1)S(1)} collective-permute-done((bf16[8,128,128]{2,1,0:T(8,128)(2,1)S(1)}, bf16[8,128,128]{2,1,0:T(8,128)(2,1)S(1)}, u32[]{:S(2)}, u32[]{:S(2)}) %collective-permute-start.6) | collective-permute-done | bytes 262176 | tf_op jit(solution)/shard_map/ppermute | solution.py:609
  94.4 19.4 %finish.1 = bf16[1024,128]{1,0:T(8,128)(2,1)S(1)} custom-call(bf16[8,128,128]{2,1,0:T(8,128)(2,1)S(1)} %apply.6.after.refs_0_, bf16[24,128,128]{2,1,0:T(8,128)(2,1)S(1)} %apply.7.refs_1_, bf16[8,128,128]{2,1,0:T(8,128)(2,1)S(1)} %collective-permute-done.6.refs_2_, f32[8,128]{1,0:T(8,128)S(1)} %get-tuple-element.19.refs_3_), custom_call_target="tpu_custom_call" | custom-call | tf_op jit(solution)/shard_map/finish/pallas_call | solution.py:621
  113.8 0.7 copy.10
  114.5 0.7 copy.11
Async XLA Ops:
  0.6 12.8 %collective-permute-start.1 = (s32[2,1024,128]{2,1,0:T(8,128)}, s32[2,1024,128]{2,1,0:T(8,128)}, u32[]{:S(2)}, u32[]{:S(2)}) collective-permute-start(s32[2,1024,128]{2,1,0:T(8,128)} %bitcast.7), channel_id=1, source_target_pairs={{0,1},{1,0},{2,3},{3,2},{4,5},{5,4},{6,7},{7,6},{8,9},{9,8},{10,11... | collective-permute-start | bytes 3145736 | tf_op jit(solution)/shard_map/ppermute | solution.py:508
  4.7 17.8 %copy-start = (bf16[8,128,128]{2,1,0:T(8,128)(2,1)S(1)}, bf16[8,128,128]{2,1,0:T(8,128)(2,1)}, u32[]{:S(2)}) copy-start(bf16[8,128,128]{2,1,0:T(8,128)(2,1)} %get-tuple-element.17.refs_0_) | copy-start | bytes 786436
  4.7 31.8 %copy-start.1 = (s32[1,1536]{1,0:T(1,128)S(1)}, s32[1,1536]{1,0:T(1,128)}, u32[]{:S(2)}) copy-start(s32[1,1536]{1,0:T(1,128)} %get-tuple-element.12.order_ref.order_a) | copy-start | bytes 18436
  4.7 14.4 %collective-permute-start.4 = (bf16[8,128,128]{2,1,0:T(8,128)(2,1)}, bf16[8,128,128]{2,1,0:T(8,128)(2,1)S(1)}, u32[]{:S(2)}, u32[]{:S(2)}) collective-permute-start(bf16[8,128,128]{2,1,0:T(8,128)(2,1)} %get-tuple-element.17.refs_0_), channel_id=1, source_target_pairs={{0,24},{8,0},{16,8},{24,16},{1,25},{9,1},{17,9},{25,17},{2,26},{10... | collective-permute-start | bytes 786440 | tf_op jit(solution)/shard_map/ppermute | solution.py:528
  8.2 14.3 %collective-permute-start.3 = (bf16[8,128,128]{2,1,0:T(8,128)(2,1)}, bf16[8,128,128]{2,1,0:T(8,128)(2,1)S(1)}, u32[]{:S(2)}, u32[]{:S(2)}) collective-permute-start(bf16[8,128,128]{2,1,0:T(8,128)(2,1)} %get-tuple-element.17.refs_0_), channel_id=1, source_target_pairs={{0,16},{8,24},{16,0},{24,8},{1,17},{9,25},{17,1},{25,9},{2,18},{10... | collective-permute-start | bytes 786440 | tf_op jit(solution)/shard_map/ppermute | solution.py:528
  8.7 13.8 %collective-permute-start.2 = (bf16[8,128,128]{2,1,0:T(8,128)(2,1)}, bf16[8,128,128]{2,1,0:T(8,128)(2,1)S(1)}, u32[]{:S(2)}, u32[]{:S(2)}) collective-permute-start(bf16[8,128,128]{2,1,0:T(8,128)(2,1)} %get-tuple-element.17.refs_0_), channel_id=1, source_target_pairs={{0,8},{8,16},{16,24},{24,0},{1,9},{9,17},{17,25},{25,1},{2,10},{10... | collective-permute-start | bytes 786440 | tf_op jit(solution)/shard_map/ppermute | solution.py:528
  9.3 4.2 %collective-permute-start = (s32[1,1536]{1,0:T(1,128)}, s32[1,1536]{1,0:T(1,128)S(1)}, u32[]{:S(2)}, u32[]{:S(2)}) collective-permute-start(s32[1,1536]{1,0:T(1,128)} %get-tuple-element.12.order_ref.order_a), channel_id=1, source_target_pairs={{0,1},{1,0},{2,3},{3,2},{4,5},{5,4},{6,7},{7,6},{8,9},{9,8},{10,11... | collective-permute-start | bytes 18440 | tf_op jit(solution)/shard_map/ppermute | solution.py:531
  13.5 0.6 copy-start.2
  22.5 0.7 copy-start.5
  36.5 0.7 copy-start.3
  41.1 35.8 %copy-start.4 = (s32[1,1536]{1,0:T(1,128)S(1)}, s32[1,1536]{1,0:T(1,128)}, u32[]{:S(2)}) copy-start(s32[1,1536]{1,0:T(1,128)} %copy-done.2) | copy-start | bytes 18436
  41.1 8.3 %collective-permute-start.5 = (bf16[8,128,128]{2,1,0:T(8,128)(2,1)S(1)}, bf16[8,128,128]{2,1,0:T(8,128)(2,1)S(1)}, u32[]{:S(2)}, u32[]{:S(2)}) collective-permute-start(bf16[8,128,128]{2,1,0:T(8,128)(2,1)S(1)} %apply.4.after.refs_0_), channel_id=1, source_target_pairs={{0,2},{1,3},{6,4},{7,5},{8,10},{9,11},{14,12},{15,13},{16,18},{17,... | collective-permute-start | bytes 786440 | tf_op jit(solution)/shard_map/ppermute | solution.py:609
  80.8 13.6 %collective-permute-start.6 = (bf16[8,128,128]{2,1,0:T(8,128)(2,1)S(1)}, bf16[8,128,128]{2,1,0:T(8,128)(2,1)S(1)}, u32[]{:S(2)}, u32[]{:S(2)}) collective-permute-start(bf16[8,128,128]{2,1,0:T(8,128)(2,1)S(1)} %apply.6.after.refs_0_), channel_id=1, source_target_pairs={{0,2},{1,3},{6,4},{7,5},{8,10},{9,11},{14,12},{15,13},{16,18},{17,... | collective-permute-start | bytes 786440 | tf_op jit(solution)/shard_map/ppermute | solution.py:609
where the time goes:
time: 117 us; the launch traced here: 115 us
  Pallas kernels  89.4 us (76%)
  starting transfers between devices  15.2 us (13%)
  waiting for transfers between devices  5.81 us (5%)
  local copies, waits for them, and re-layouts  3.4 us (3%)
  between operations  1.47 us (1%)
    pallas_call x2, Pallas kernels, collect(): pl.pallas_call(functools.partial(sum_kernel, n_row, n_col, spread), out_s...  46.8 us
    pallas_call x4, Pallas kernels, apply(): pl.pallas_call(body, in_specs=[SMEM_SPEC] * 2 + [ANY_SPEC] * 2 + [VMEM_SP...  17.3 us
    pallas_call x1, Pallas kernels, local(): pl.pallas_call(functools.partial(start_kernel, n_row, n_col), out_shape=[...  13.3 us
    ppermute x2, starting transfers between devices, apply_all(): given.append(lax.ppermute(parts[-1], 'col', ends))  10.1 us
    pallas_call x2, Pallas kernels, build(): pl.pallas_call(functools.partial(build_kernel, half_tiles, len(previous))...  9.18 us
    ppermute x3, starting transfers between devices, local(): lax.ppermute(turned, 'row', [(i, (i + d) % n_row) for i in range(n_row)])  4.59 us
    unnamed x14, local copies, waits for them, and re-layouts  3.4 us
    ppermute x3, waiting for transfers between devices, local(): lax.ppermute(turned, 'row', [(i, (i + d) % n_row) for i in range(n_row)])  3.35 us
  transfers between devices with their start and end apart: 7, of which 3 were waited for; matrix products, arithmetic and copies ran while one was open for 0% of the time, Pallas kernels for 19%

commit v1 on v0

--- a/solution.py
+++ b/solution.py
@@ -10,7 +10,9 @@
 TILE = 128
 ROWS_MIN = 16
 BUILD_UNROLL = 32
-BUILD_SLOTS = 6
+BUILD_SLOTS = 1
+KEPT_PAIRS = 416
+LATE_PAIRS = 8
 APPLY_UNROLL = 64
 APPLY_SLOTS = 4
 HOT = jnp.float8_e4m3fn
@@ -118,12 +120,32 @@
     return order_ref[0, base], order_ref[0, base + first], order_ref[0, base + last]
 
 
-def build_kernel(half_bins, other, order_ref, edges_ref, *refs):
-    *previous, store_ref, degree_ref, made, degree_acc, sem = refs
+def lists_of(orders, total_pairs, half_bins, first, last):
+    pairs = BUILD_UNROLL // 2
+    spans, start = [], 0
+    for other, order_ref in enumerate(orders):
+        low, begin, end = spans_of(order_ref, total_pairs, half_bins, other, first, last)
+        spans.append((start - low, begin, end))
+        high = spans_of(order_ref, total_pairs, half_bins, other, 0, half_bins)[2]
+        start = start + (high - low + pairs - 1) // pairs * pairs
+    return spans, start // pairs
+
+
+def build_kernel(
+    half_bins, total_pairs, order_a, order_b, edges_a, edges_b, kept_ref, store_ref, degree_ref,
+    edges_ref, made, degree_acc, sem, edge_sem
+):
+    loads = [
+        pltpu.make_async_copy(source, edges_ref.at[i], edge_sem.at[i])
+        for i, source in enumerate((edges_a, edges_b))
+    ]
+    for load in loads:
+        load.start()
     degree_acc[...] = jnp.zeros_like(degree_acc)
-    _, low, high = spans_of(order_ref, store_ref.shape[0], half_bins, other, 0, half_bins)
     pairs = BUILD_UNROLL // 2
-    turns = (high - low + pairs - 1) // pairs
+    (span_a, span_b), turns = lists_of((order_a, order_b), total_pairs, half_bins, 0, half_bins)
+    turns_a = (span_b[0] + span_b[1]) // pairs
+    kept_turns = jnp.minimum(turns, KEPT_PAIRS // pairs)
     mask = 2**SLOT_BITS - 1
     cells = [
         (lax.broadcasted_iota(jnp.int32, (HOT_ROWS, TILE), 0) + start).astype(jnp.int8)
@@ -136,106 +158,103 @@
             [jnp.where(ids == cell, HOT(1), HOT(0)) for cell in cells], axis=0
         )
 
+    def fill(turn, target):
+        mine = turn < turns_a
+        other = jnp.where(mine, 0, 1)
+        high = jnp.where(mine, span_a[2], span_b[2])
+        low = turn * pairs - jnp.where(mine, 0, span_b[0])
+        for pair in range(pairs):
+            counts = []
+            base = low + pair
+            code = jnp.where(mine, order_a[0, base], order_b[0, base])
+            live = jnp.where(base < high, code, 0)
+            for half in range(2):
+                slot = ((live >> (half * SLOT_BITS)) & mask) - 1
+                safe = jnp.maximum(slot, 0)
+                dst = jnp.where(slot >= 0, edges_ref[other, 0, pl.ds(safe, 1), :], -1)
+                src = edges_ref[other, 1, pl.ds(safe, 1), :]
+                both = lax.dot_general(
+                    hot(src), hot(dst), (((1,), (1,)), ((), ())), preferred_element_type=jnp.float32
+                )
+                target[pair, half * TILE : (half + 1) * TILE] = both.astype(jnp.bfloat16)
+                counts.append(jnp.sum(both.reshape(TILE // 8, 8, TILE), axis=0))
+            degree_acc[live >> (2 * SLOT_BITS)] += counts[0] + counts[1]
+
+    def keep(turn, carry):
+        fill(turn, kept_ref.at[pl.ds(turn * pairs, pairs)])
+        return carry
+
+    for load in loads:
+        load.wait()
+    lax.fori_loop(0, kept_turns, keep, 0)
+
     def out_copy(turn):
         side = lax.rem(turn, BUILD_SLOTS)
         return pltpu.make_async_copy(
             made.at[side], store_ref.at[pl.ds(turn * pairs, pairs)], sem.at[side]
         )
 
-    def visit(turn, carry):
-        side = lax.rem(turn, BUILD_SLOTS)
-
-        @pl.when(turn >= BUILD_SLOTS)
+    def spill(turn, carry):
+        @pl.when(turn >= kept_turns + BUILD_SLOTS)
         def _():
             out_copy(turn - BUILD_SLOTS).wait()
 
-        for pair in range(pairs):
-            counts = []
-            base = low + turn * pairs + pair
-            code = order_ref[0, base]
-            live = jnp.where(base < high, code, 0)
-            for half in range(2):
-                slot = ((live >> (half * SLOT_BITS)) & mask) - 1
-                safe = jnp.maximum(slot, 0)
-                dst = jnp.where(slot >= 0, edges_ref[0, pl.ds(safe, 1), :], -1)
-                src = edges_ref[1, pl.ds(safe, 1), :]
-                both = lax.dot_general(
-                    hot(src), hot(dst), (((1,), (1,)), ((), ())), preferred_element_type=jnp.float32
-                )
-                made[side, pair, half * TILE : (half + 1) * TILE] = both.astype(jnp.bfloat16)
-                counts.append(jnp.sum(both.reshape(TILE // 8, 8, TILE), axis=0))
-            degree_acc[live >> (2 * SLOT_BITS)] += counts[0] + counts[1]
+        fill(turn, made.at[lax.rem(turn, BUILD_SLOTS)])
         out_copy(turn).start()
         return carry
 
-    lax.fori_loop(0, turns, visit, 0)
-
+    lax.fori_loop(kept_turns, turns, spill, 0)
     for back in range(BUILD_SLOTS, 0, -1):
 
-        @pl.when(turns >= back)
+        @pl.when(turns - back >= kept_turns)
         def _():
             out_copy(turns - back).wait()
 
-    degree = jnp.sum(degree_acc[...], axis=1)
-    degree_ref[...] = degree + previous[0][...] if previous else degree
-
-
-def apply_kernel(half_bins, first_row, orders, stores, source_ref, out_ref, held, acc, sem):
+    degree_ref[...] = jnp.sum(degree_acc[...], axis=1)
+
+
+def apply_kernel(half_bins, total_pairs, first_row, orders, kept_ref, store_ref, source_ref, out_ref, held, acc, sem):
+    acc[...] = jnp.zeros_like(acc)
     rows = out_ref.shape[0]
-    pairs = APPLY_UNROLL // 2
-    total_pairs = stores[0].shape[0]
-    lists, spans, turns = [], [], []
+    code_mask = 2**CODE_BITS - 1
+    spans, _ = lists_of(orders, total_pairs, half_bins, first_row, first_row + rows)
+
     for other, order_ref in enumerate(orders):
-        start, low, high = spans_of(
-            order_ref, total_pairs, half_bins, other, first_row, first_row + rows
-        )
-        lists.append(start)
-        spans.append((low, high))
-        turns.append((high - low + pairs - 1) // pairs)
-    code_mask = 2**CODE_BITS - 1
-
-    def fetch(turn):
-        slot = lax.rem(turn, APPLY_SLOTS)
-        for other in range(2):
-            local = turn - other * turns[0]
-
-            @pl.when((local >= 0) & (local < turns[other]))
-            def _():
-                start = spans[other][0] - lists[other] + local * pairs
-                pltpu.make_async_copy(
-                    stores[other].at[pl.ds(start, pairs)], held.at[slot], sem.at[slot]
-                ).start()
-
-    for turn in range(APPLY_SLOTS - 1):
-        fetch(turn)
-    acc[...] = jnp.zeros_like(acc)
-
-    for other in range(2):
-        order_ref = orders[other]
-        low, high = spans[other]
+        shift, low, high = spans[other]
         offset = other * source_ref.shape[0] // 2
+        edge = jnp.minimum(high, KEPT_PAIRS - shift)
+        late = jnp.maximum(low, KEPT_PAIRS - shift)
+
+        def add(base, end, tile):
+            code = order_ref[0, total_pairs + base]
+            left = (code >> CODE_BITS) & code_mask
+            right = code >> (2 * CODE_BITS)
+            sources = jnp.concatenate(
+                [source_ref[offset + left], source_ref[offset + right]], axis=1
+            )
+            place = jnp.where(base < end, (code & code_mask) - first_row, rows)
+            acc[place] += jnp.dot(sources, tile, preferred_element_type=jnp.float32)
 
         def visit(turn, carry):
-            slot = lax.rem(turn, APPLY_SLOTS)
-            pltpu.make_async_copy(
-                stores[0].at[pl.ds(0, pairs)], held.at[slot], sem.at[slot]
-            ).wait()
-            fetch(turn + APPLY_SLOTS - 1)
-            for pair in range(pairs):
-                base = low + (turn - other * turns[0]) * pairs + pair
-                code = order_ref[0, total_pairs + base]
-                left = (code >> CODE_BITS) & code_mask
-                right = code >> (2 * CODE_BITS)
-                sources = jnp.concatenate(
-                    [source_ref[offset + left], source_ref[offset + right]], axis=1
-                )
-                place = jnp.where(base < high, (code & code_mask) - first_row, rows)
-                acc[place] += jnp.dot(
-                    sources, held[slot, pair], preferred_element_type=jnp.float32
-                )
+            for pair in range(APPLY_UNROLL // 2):
+                base = low + turn * (APPLY_UNROLL // 2) + pair
+                add(base, edge, kept_ref[base + shift])
             return carry
 
-        lax.fori_loop(other * turns[0], turns[0] + other * turns[1], visit, 0)
+        lax.fori_loop(0, (edge - low + APPLY_UNROLL // 2 - 1) // (APPLY_UNROLL // 2), visit, 0)
+
+        def visit_late(turn, carry):
+            first = late + turn * LATE_PAIRS
+            copy = pltpu.make_async_copy(
+                store_ref.at[pl.ds(first + shift, LATE_PAIRS)], held, sem
+            )
+            copy.start()
+            copy.wait()
+            for pair in range(LATE_PAIRS):
+                add(first + pair, high, held[pair])
+            return carry
+
+        lax.fori_loop(0, (high - late + LATE_PAIRS - 1) // LATE_PAIRS, visit_late, 0)
     out_ref[...] = acc[:rows].astype(jnp.bfloat16)
 
 
@@ -379,7 +398,7 @@
             (row, lax.rem(col + jnp.where(way == 0, CORES, n_col - CORES), n_col)),
         )
 
-    flow = [(k, piece) for piece in range(PIECES) for k in range(last)]
+    flow = [(k, piece) for k in range(last) for piece in range(PIECES)]
     timed = [(i, 0, *f) for i, f in enumerate(flow)]
     timed += [(i + RELAY_LAG, 1, *f) for i, f in enumerate(flow) if f[0] < n_chip // 2 - 1]
 
@@ -473,9 +492,9 @@
     return pltpu.SemaphoreType.DMA(shape)
 
 
-def comm_params(ident):
+def comm_params(ident, scratch):
     return pltpu.CompilerParams(
-        collective_id=ident, has_side_effects=True, vmem_limit_bytes=48 * 2**20
+        collective_id=ident, has_side_effects=True, vmem_limit_bytes=scratch + 2**20
     )
 
 
@@ -483,12 +502,8 @@
     return pltpu.CompilerParams(vmem_limit_bytes=67043328)
 
 
-def build_params():
-    return pltpu.CompilerParams(vmem_limit_bytes=65 * 10**6)
-
-
-def plain_params():
-    return pltpu.CompilerParams(vmem_limit_bytes=48 * 2**20)
+def plain_params(scratch):
+    return pltpu.CompilerParams(vmem_limit_bytes=scratch + 2**20)
 
 
 def local(features, tile_rows, tile_cols, edge_lists, tile_counts):
@@ -500,6 +515,7 @@
     source_tiles = own * n_row
     slots = tile_rows.shape[-1]
     bf16, f32 = jnp.bfloat16, jnp.float32
+    tile_bytes = feat_width * TILE * 2
     spare = max(BUILD_UNROLL, APPLY_UNROLL)
     pairs = -(-(slots + CORES * half_tiles + spare) // (2 * TILE)) * TILE
     swap = [(i, i + 1 - 2 * (i % CORES)) for i in range(n_col)]
@@ -530,27 +546,26 @@
     ]
     order_b = lax.ppermute(order, "col", swap)
 
-    def build(order, edges, *previous):
-        return pl.pallas_call(
-            functools.partial(build_kernel, half_tiles, len(previous)),
-            in_specs=[SMEM_SPEC, VMEM_SPEC] + [VMEM_SPEC] * len(previous),
-            out_specs=[ANY_SPEC, VMEM_SPEC],
-            scratch_shapes=[
-                pltpu.VMEM((BUILD_SLOTS, BUILD_UNROLL // 2, 2 * TILE, TILE), bf16),
-                pltpu.VMEM((half_tiles, 8, TILE), f32),
-                sems(BUILD_SLOTS),
-            ],
-            out_shape=[
-                jax.ShapeDtypeStruct((pairs, 2 * TILE, TILE), bf16),
-                jax.ShapeDtypeStruct((half_tiles, TILE), f32),
-            ],
-            compiler_params=build_params(),
-            cost_estimate=pl.CostEstimate(flops=10**10, bytes_accessed=0, transcendentals=0),
-            name="build",
-        )(order, edges, *previous)
-
-    store_a, degree_a = build(order, edges)
-    store_b, degree = build(order_b, edges_b, degree_a)
+    kept, store, degree = pl.pallas_call(
+        functools.partial(build_kernel, half_tiles, pairs),
+        in_specs=[SMEM_SPEC] * 2 + [HBM_SPEC] * 2,
+        out_specs=[VMEM_SPEC, ANY_SPEC, VMEM_SPEC],
+        scratch_shapes=[
+            pltpu.VMEM((2, 2, slots, TILE), jnp.int32),
+            pltpu.VMEM((BUILD_SLOTS, BUILD_UNROLL // 2, 2 * TILE, TILE), bf16),
+            pltpu.VMEM((half_tiles, 8, TILE), f32),
+            sems(BUILD_SLOTS),
+            sems(2),
+        ],
+        out_shape=[
+            jax.ShapeDtypeStruct((KEPT_PAIRS + APPLY_UNROLL // 2, 2 * TILE, TILE), bf16),
+            jax.ShapeDtypeStruct((2 * pairs, 2 * TILE, TILE), bf16),
+            jax.ShapeDtypeStruct((half_tiles, TILE), f32),
+        ],
+        compiler_params=plain_params(4 * slots * TILE * 4 + BUILD_UNROLL * TILE * TILE * 2),
+        cost_estimate=pl.CostEstimate(flops=10**10, bytes_accessed=0, transcendentals=0),
+        name="build",
+    )(order, order_b, edges, edges_b)
 
     gathered_type = jax.ShapeDtypeStruct((CORES * source_tiles, feat_width, TILE), bf16)
     gathered, root = pl.pallas_call(
@@ -569,32 +584,53 @@
             sems(2, n_row),
             sems(2, n_row),
         ],
-        compiler_params=comm_params(0),
+        compiler_params=comm_params(0, n_row * own * tile_bytes),
         name="start",
     )(degree, *blocks)
 
-    def apply(sources, ranks, after):
+    def apply(sources, ranks, after, hop=None):
         rows = len(ranks) * own
-
-        def body(order_a, order_b, store_a, store_b, sources, after, *refs):
+        hops = [] if hop is None else [hop]
+
+        def body(order_a, order_b, kept, store, sources, after, *refs):
+            if hops:
+                hop_ref, out_ref, hop_out, *scratch, hop_sem = refs
+                copy = pltpu.make_async_copy(hop_ref, hop_out, hop_sem)
+                copy.start()
+            else:
+                out_ref, *scratch = refs
             apply_kernel(
-                half_tiles, ranks[0] * own, (order_a, order_b), (store_a, store_b), sources, *refs
-            )
+                half_tiles,
+                pairs,
+                ranks[0] * own,
+                (order_a, order_b),
+                kept,
+                store,
+                sources,
+                out_ref,
+                *scratch,
+            )
+            if hops:
+                copy.wait()
 
         return pl.pallas_call(
             body,
-            in_specs=[SMEM_SPEC] * 2 + [ANY_SPEC] * 2 + [VMEM_SPEC, ANY_SPEC],
-            out_specs=VMEM_SPEC,
+            in_specs=[SMEM_SPEC] * 2
+            + [VMEM_SPEC, ANY_SPEC] * 2
+            + [VMEM_SPEC] * len(hops),
+            out_specs=[VMEM_SPEC] + [ANY_SPEC] * len(hops),
             scratch_shapes=[
-                pltpu.VMEM((APPLY_SLOTS, APPLY_UNROLL // 2, 2 * TILE, TILE), bf16),
+                pltpu.VMEM((LATE_PAIRS, 2 * TILE, TILE), bf16),
                 pltpu.VMEM((rows + 1, feat_width, TILE), f32),
-                sems(APPLY_SLOTS),
-            ],
-            out_shape=jax.ShapeDtypeStruct((rows, feat_width, TILE), bf16),
-            compiler_params=plain_params(),
+                pltpu.SemaphoreType.DMA,
+            ]
+            + [pltpu.SemaphoreType.DMA] * len(hops),
+            out_shape=[jax.ShapeDtypeStruct((rows, feat_width, TILE), bf16)]
+            + [jax.ShapeDtypeStruct(hop.shape, hop.dtype) for hop in hops],
+            compiler_params=plain_params((2 * rows + 2 + 2 * LATE_PAIRS) * tile_bytes),
             cost_estimate=pl.CostEstimate(flops=10**10, bytes_accessed=0, transcendentals=0),
             name="apply",
-        )(order, order_b, store_a, store_b, sources, after)
+        )(order, order_b, kept, store, sources, after, *hops)
 
     ends = [
         (a * CORES + core, b * CORES + core)
@@ -602,14 +638,15 @@
         for core in range(CORES)
     ]
 
-    def apply_all(sources):
+    def apply_all(sources, hop=None):
         parts, given, after = [], [], sources
         for rank in range(EARLY):
-            parts.append(apply(sources, [rank], after))
-            given.append(lax.ppermute(parts[-1], "col", ends))
-            after = parts[-1]
-        parts.append(apply(sources, list(range(EARLY, n_chip)), after))
-        return parts + given
+            (part,) = apply(sources, [rank], after)
+            parts.append(part)
+            given.append(lax.ppermute(part, "col", ends))
+            after = part
+        part, *hops = apply(sources, list(range(EARLY, n_chip)), after, hop)
+        return parts + [part] + given, *hops
 
     def collect(parts, spread):
         size = own // PIECES
@@ -625,12 +662,16 @@
             out_specs=[VMEM_SPEC] * len(outs),
             scratch_shapes=[pltpu.VMEM((2, n_chip - 1, PIECES, size, feat_width, TILE), bf16)] * 2
             + semaphores,
-            compiler_params=comm_params(1 if spread else 2),
+            compiler_params=comm_params(
+                1 if spread else 2, 4 * (n_chip - 1) * own * tile_bytes
+            ),
             name="spread" if spread else "finish",
         )(*parts, root)
 
-    hop_one, gathered = collect(apply_all(gathered), True)
-    (hop_two,) = collect(apply_all(gathered), False)
+    (parts,) = apply_all(gathered)
+    hop_one, gathered = collect(parts, True)
+    parts, hop_one = apply_all(gathered, hop_one)
+    (hop_two,) = collect(parts, False)
     return (hop_one, hop_two)
 
 

time: 117 us -> 97.1 us (0.83); the launches traced: 115 us -> 98.8 us
  Pallas kernels: 89.4 us -> 76.3 us
  starting transfers between devices: 15.2 us -> 12.4 us
    pallas_call x2, Pallas kernels: 46.8 us -> 38.5 us  [collect(): pl.pallas_call(functools.partial(sum_kernel, n_row, n_col, spread), out_s...]
    pallas_call x6 -> x5, Pallas kernels: 26.4 us -> 22.8 us  [the longest x4 15.7 us: apply(): pl.pallas_call(body, in_specs=[SMEM_SPEC] * 2 + [VMEM_SPEC, ANY_SPEC] * 2...]
    ppermute x2, starting transfers between devices: 10.1 us -> 6.79 us  [apply_all(): given.append(lax.ppermute(part, 'col', ends))]
    unnamed x14 -> x9, local copies, waits for them, and re-layouts: 3.4 us -> 2.63 us
  transfers between devices with their start and end apart: 7 -> 7, of which waited for: 3 -> 3; matrix products, arithmetic and copies ran while one was open for 0% -> 0% of each run, Pallas kernels for 19% -> 20%
where the time goes in v1:
time: 97.1 us; the launch traced here: 98.8 us
  Pallas kernels  76.3 us (79%)
  starting transfers between devices  12.4 us (13%)
  waiting for transfers between devices  6.06 us (6%)
  local copies, waits for them, and re-layouts  2.63 us (3%)
  between operations  1.41 us (1%)
    pallas_call x2, Pallas kernels, collect(): pl.pallas_call(functools.partial(sum_kernel, n_row, n_col, spread), out_s...  38.5 us
    pallas_call x4, Pallas kernels, apply(): pl.pallas_call(body, in_specs=[SMEM_SPEC] * 2 + [VMEM_SPEC, ANY_SPEC] * 2...  15.7 us
    pallas_call x1, Pallas kernels, local(): pl.pallas_call(functools.partial(start_kernel, n_row, n_col), out_shape=[...  12.2 us
    pallas_call x1, Pallas kernels, local(): pl.pallas_call(functools.partial(build_kernel, half_tiles, pairs), in_spe...  7.11 us
    ppermute x2, starting transfers between devices, apply_all(): given.append(lax.ppermute(part, 'col', ends))  6.79 us
    ppermute x3, starting transfers between devices, local(): lax.ppermute(turned, 'row', [(i, (i + d) % n_row) for i in range(n_row)])  5.01 us
    ppermute x3, waiting for transfers between devices, local(): lax.ppermute(turned, 'row', [(i, (i + d) % n_row) for i in range(n_row)])  3.68 us
    pallas_call x1, Pallas kernels, local(): pl.pallas_call(functools.partial(order_kernel, own, n_chip, pairs), out_s...  2.83 us
  transfers between devices with their start and end apart: 7, of which 3 were waited for; matrix products, arithmetic and copies ran while one was open for 0% of the time, Pallas kernels for 20%

profile of v1, /device:TPU:0, one launch (start us, length us, event | category | flops | bytes accessed | tf_op | source)
XLA Modules:
  0.0 98.8 jit_solution(5122815212497633858)
XLA Ops:
  0.6 0.6 collective-permute-start.1
  1.8 2.8 %order.1 = (s32[1,1536]{1,0:T(1,128)}, bf16[8,128,128]{2,1,0:T(8,128)(2,1)}) custom-call(s32[1]{0:T(128)} %bitcast.4.count_ref, s32[1,1024]{1,0:T(1,128)} %bitcast.7, s32[1,1024]{1,0:T(1,128)} %bitcast.8, bf16[1024,128]{1,0:T(8,128)(2,1)} %features_hbm.1), custom_call_target="tpu_custom_call" | custom-call | tf_op jit(solution)/shard_map/order/pallas_call | solution.py:526
  4.7 0.0 copy-start
  4.7 0.1 collective-permute-start
  4.8 3.9 %collective-permute-start.4 = (bf16[8,128,128]{2,1,0:T(8,128)(2,1)}, bf16[8,128,128]{2,1,0:T(8,128)(2,1)S(1)}, u32[]{:S(2)}, u32[]{:S(2)}) collective-permute-start(bf16[8,128,128]{2,1,0:T(8,128)(2,1)} %get-tuple-element.17.refs_0_), channel_id=1, source_target_pairs={{0,24},{8,0},{16,8},{24,16},{1,25},{9,1},{17,9},{25,17},{2,26},{10... | collective-permute-start | bytes 786440 | tf_op jit(solution)/shard_map/ppermute | solution.py:544
  8.7 0.5 collective-permute-start.3
  9.2 0.6 collective-permute-start.2
  9.8 0.0 collective-permute-done.order_b
  9.8 0.0 collective-permute-done.1.edges_b
  9.8 0.0 copy-start.1
  9.8 0.7 copy-done.1
  10.5 0.0 copy-start.3
  10.5 1.2 %copy-done.3 = s32[2,1,1,1024,128]{4,3,2,1,0:T(8,128)S(1)} copy-done((s32[2,1,1,1024,128]{4,3,2,1,0:T(8,128)S(1)}, s32[2,1,1,1024,128]{4,3,2,1,0:T(8,128)}, u32[]{:S(2)}) %copy-start.3) | copy-done | bytes 1048600
  11.7 7.1 %build.1 = (bf16[448,256,128]{2,1,0:T(8,128)(2,1)S(1)}, bf16[1280,256,128]{2,1,0:T(8,128)(2,1)}, f32[32,128]{1,0:T(8,128)S(1)}) custom-call(s32[1,1536]{1,0:T(1,128)S(1)} %copy-done.1, s32[1,1536]{1,0:T(1,128)S(1)} %collective-permute-done.order_b, s32[2,1024,128]{2,1,0:T(8,128)S(1)} %bitcast.6, s32[2,1024,128]{2,1,0:T(8,128)} %collective-permute-done.1.edges_b), custom_call_target="tpu_custom_call" | custom-call | flops 10000000000 | tf_op jit(solution)/shard_map/build/pallas_call | solution.py:549
  18.8 0.0 collective-permute-done.4.refs_3_
  18.8 3.7 %collective-permute-done.3.refs_2_ = bf16[8,128,128]{2,1,0:T(8,128)(2,1)S(1)} collective-permute-done((bf16[8,128,128]{2,1,0:T(8,128)(2,1)}, bf16[8,128,128]{2,1,0:T(8,128)(2,1)S(1)}, u32[]{:S(2)}, u32[]{:S(2)}) %collective-permute-start.3) | collective-permute-done | bytes 262176 | tf_op jit(solution)/shard_map/ppermute | solution.py:544
  22.5 0.0 collective-permute-done.2.refs_1_
  22.5 0.0 copy-done
  22.5 12.2 %start.1 = (bf16[64,128,128]{2,1,0:T(8,128)(2,1)S(1)}, f32[8,128]{1,0:T(8,128)S(1)}) custom-call(f32[32,128]{1,0:T(8,128)S(1)} %get-tuple-element.16.part, bf16[8,128,128]{2,1,0:T(8,128)(2,1)S(1)} %copy-done, bf16[8,128,128]{2,1,0:T(8,128)(2,1)S(1)} %collective-permute-done.2.refs_1_, bf16[8,128,128]{2,1,0:T(8,128)(2,1)S(1)} %collective-permute-done.3.refs_2_, ...), custom_call_target="tpu_custom_call" | custom-call | tf_op jit(solution)/shard_map/start/pallas_call | solution.py:571
  34.7 0.0 copy-start.2
  34.8 3.1 %apply.4.after.refs_0_ = bf16[8,128,128]{2,1,0:T(8,128)(2,1)S(1)} custom-call(s32[1,1536]{1,0:T(1,128)S(1)} %copy-done.1, s32[1,1536]{1,0:T(1,128)S(1)} %collective-permute-done.order_b, bf16[448,256,128]{2,1,0:T(8,128)(2,1)S(1)} %get-tuple-element.14.kept, bf16[1280,256,128]{2,1,0:T(8,128)(2,1)} %get-tuple-element.15.store, ...), custom_call_target="tpu_custom_call" | custom-call | flops 10000000000 | tf_op jit(solution)/shard_map/apply/pallas_call | solution.py:616
  37.9 1.8 %collective-permute-start.5 = (bf16[8,128,128]{2,1,0:T(8,128)(2,1)S(1)}, bf16[8,128,128]{2,1,0:T(8,128)(2,1)S(1)}, u32[]{:S(2)}, u32[]{:S(2)}) collective-permute-start(bf16[8,128,128]{2,1,0:T(8,128)(2,1)S(1)} %apply.4.after.refs_0_), channel_id=1, source_target_pairs={{0,2},{1,3},{6,4},{7,5},{8,10},{9,11},{14,12},{15,13},{16,18},{17,... | collective-permute-start | bytes 786440 | tf_op jit(solution)/shard_map/ppermute | solution.py:646
  39.7 0.0 copy-done.2
  39.7 4.7 %apply.5.refs_1_ = bf16[24,128,128]{2,1,0:T(8,128)(2,1)S(1)} custom-call(s32[1,1536]{1,0:T(1,128)S(1)} %copy-done.2, s32[1,1536]{1,0:T(1,128)S(1)} %collective-permute-done.order_b, bf16[448,256,128]{2,1,0:T(8,128)(2,1)S(1)} %get-tuple-element.14.kept, bf16[1280,256,128]{2,1,0:T(8,128)(2,1)} %get-tuple-element.15.store, ...), custom_call_target="tpu_custom_call" | custom-call | flops 10000000000 | tf_op jit(solution)/shard_map/apply/pallas_call | solution.py:616
  44.4 1.0 %collective-permute-done.5.refs_2_ = bf16[8,128,128]{2,1,0:T(8,128)(2,1)S(1)} collective-permute-done((bf16[8,128,128]{2,1,0:T(8,128)(2,1)S(1)}, bf16[8,128,128]{2,1,0:T(8,128)(2,1)S(1)}, u32[]{:S(2)}, u32[]{:S(2)}) %collective-permute-start.5) | collective-permute-done | bytes 262176 | tf_op jit(solution)/shard_map/ppermute | solution.py:646
  45.4 24.0 %spread.1 = (bf16[1024,128]{1,0:T(8,128)(2,1)S(1)}, bf16[64,128,128]{2,1,0:T(8,128)(2,1)S(1)}) custom-call(bf16[8,128,128]{2,1,0:T(8,128)(2,1)S(1)} %apply.4.after.refs_0_, bf16[24,128,128]{2,1,0:T(8,128)(2,1)S(1)} %apply.5.refs_1_, bf16[8,128,128]{2,1,0:T(8,128)(2,1)S(1)} %collective-permute-done.5.refs_2_, f32[8,128]{1,0:T(8,128)S(1)} %get-tuple-element.19.refs_3_), custom_call_target="tpu_custom_call" | custom-call | tf_op jit(solution)/shard_map/spread/pallas_call | solution.py:658
  69.4 3.1 %apply.6.after.refs_0_ = bf16[8,128,128]{2,1,0:T(8,128)(2,1)S(1)} custom-call(s32[1,1536]{1,0:T(1,128)S(1)} %copy-done.2, s32[1,1536]{1,0:T(1,128)S(1)} %collective-permute-done.order_b, bf16[448,256,128]{2,1,0:T(8,128)(2,1)S(1)} %get-tuple-element.14.kept, bf16[1280,256,128]{2,1,0:T(8,128)(2,1)} %get-tuple-element.15.store, ...), custom_call_target="tpu_custom_call" | custom-call | flops 10000000000 | tf_op jit(solution)/shard_map/apply/pallas_call | solution.py:616
  72.5 5.0 %collective-permute-start.6 = (bf16[8,128,128]{2,1,0:T(8,128)(2,1)S(1)}, bf16[8,128,128]{2,1,0:T(8,128)(2,1)S(1)}, u32[]{:S(2)}, u32[]{:S(2)}) collective-permute-start(bf16[8,128,128]{2,1,0:T(8,128)(2,1)S(1)} %apply.6.after.refs_0_), channel_id=1, source_target_pairs={{0,2},{1,3},{6,4},{7,5},{8,10},{9,11},{14,12},{15,13},{16,18},{17,... | collective-permute-start | bytes 786440 | tf_op jit(solution)/shard_map/ppermute | solution.py:646
  77.5 4.7 %apply.7 = (bf16[24,128,128]{2,1,0:T(8,128)(2,1)S(1)}, bf16[1024,128]{1,0:T(8,128)(2,1)}) custom-call(s32[1,1536]{1,0:T(1,128)S(1)} %copy-done.2, s32[1,1536]{1,0:T(1,128)S(1)} %collective-permute-done.order_b, bf16[448,256,128]{2,1,0:T(8,128)(2,1)S(1)} %get-tuple-element.14.kept, bf16[1280,256,128]{2,1,0:T(8,128)(2,1)} %get-tuple-element.15.store, ...), custom_call_target="tpu_custom_call" | custom-call | flops 10000000000 | tf_op jit(solution)/shard_map/apply/pallas_call | solution.py:616
  82.3 1.4 %collective-permute-done.6.refs_2_ = bf16[8,128,128]{2,1,0:T(8,128)(2,1)S(1)} collective-permute-done((bf16[8,128,128]{2,1,0:T(8,128)(2,1)S(1)}, bf16[8,128,128]{2,1,0:T(8,128)(2,1)S(1)}, u32[]{:S(2)}, u32[]{:S(2)}) %collective-permute-start.6) | collective-permute-done | bytes 262176 | tf_op jit(solution)/shard_map/ppermute | solution.py:646
  83.6 14.5 %finish.1 = bf16[1024,128]{1,0:T(8,128)(2,1)S(1)} custom-call(bf16[8,128,128]{2,1,0:T(8,128)(2,1)S(1)} %apply.6.after.refs_0_, bf16[24,128,128]{2,1,0:T(8,128)(2,1)S(1)} %get-tuple-element.23.refs_1_, bf16[8,128,128]{2,1,0:T(8,128)(2,1)S(1)} %collective-permute-done.6.refs_2_, f32[8,128]{1,0:T(8,128)S(1)} %get-tuple-element.19.refs_3_), custom_call_target="tpu_custom_call" | custom-call | tf_op jit(solution)/shard_map/finish/pallas_call | solution.py:658
  98.1 0.7 copy.9
Async XLA Ops:
  0.6 9.2 %collective-permute-start.1 = (s32[2,1024,128]{2,1,0:T(8,128)}, s32[2,1024,128]{2,1,0:T(8,128)}, u32[]{:S(2)}, u32[]{:S(2)}) collective-permute-start(s32[2,1024,128]{2,1,0:T(8,128)} %bitcast.5), channel_id=1, source_target_pairs={{0,1},{1,0},{2,3},{3,2},{4,5},{5,4},{6,7},{7,6},{8,9},{9,8},{10,11... | collective-permute-start | bytes 3145736 | tf_op jit(solution)/shard_map/ppermute | solution.py:524
  4.7 17.8 %copy-start = (bf16[8,128,128]{2,1,0:T(8,128)(2,1)S(1)}, bf16[8,128,128]{2,1,0:T(8,128)(2,1)}, u32[]{:S(2)}) copy-start(bf16[8,128,128]{2,1,0:T(8,128)(2,1)} %get-tuple-element.17.refs_0_) | copy-start | bytes 786436
  4.7 5.1 %collective-permute-start = (s32[1,1536]{1,0:T(1,128)}, s32[1,1536]{1,0:T(1,128)S(1)}, u32[]{:S(2)}, u32[]{:S(2)}) collective-permute-start(s32[1,1536]{1,0:T(1,128)} %get-tuple-element.13.order_a), channel_id=1, source_target_pairs={{0,1},{1,0},{2,3},{3,2},{4,5},{5,4},{6,7},{7,6},{8,9},{9,8},{10,11... | collective-permute-start | bytes 18440 | tf_op jit(solution)/shard_map/ppermute | solution.py:547
  4.8 14.1 %collective-permute-start.4 = (bf16[8,128,128]{2,1,0:T(8,128)(2,1)}, bf16[8,128,128]{2,1,0:T(8,128)(2,1)S(1)}, u32[]{:S(2)}, u32[]{:S(2)}) collective-permute-start(bf16[8,128,128]{2,1,0:T(8,128)(2,1)} %get-tuple-element.17.refs_0_), channel_id=1, source_target_pairs={{0,24},{8,0},{16,8},{24,16},{1,25},{9,1},{17,9},{25,17},{2,26},{10... | collective-permute-start | bytes 786440 | tf_op jit(solution)/shard_map/ppermute | solution.py:544
  8.7 13.8 %collective-permute-start.3 = (bf16[8,128,128]{2,1,0:T(8,128)(2,1)}, bf16[8,128,128]{2,1,0:T(8,128)(2,1)S(1)}, u32[]{:S(2)}, u32[]{:S(2)}) collective-permute-start(bf16[8,128,128]{2,1,0:T(8,128)(2,1)} %get-tuple-element.17.refs_0_), channel_id=1, source_target_pairs={{0,16},{8,24},{16,0},{24,8},{1,17},{9,25},{17,1},{25,9},{2,18},{10... | collective-permute-start | bytes 786440 | tf_op jit(solution)/shard_map/ppermute | solution.py:544
  9.2 13.3 %collective-permute-start.2 = (bf16[8,128,128]{2,1,0:T(8,128)(2,1)}, bf16[8,128,128]{2,1,0:T(8,128)(2,1)S(1)}, u32[]{:S(2)}, u32[]{:S(2)}) collective-permute-start(bf16[8,128,128]{2,1,0:T(8,128)(2,1)} %get-tuple-element.17.refs_0_), channel_id=1, source_target_pairs={{0,8},{8,16},{16,24},{24,0},{1,9},{9,17},{17,25},{25,1},{2,10},{10... | collective-permute-start | bytes 786440 | tf_op jit(solution)/shard_map/ppermute | solution.py:544
  9.8 0.7 copy-start.1
  10.5 1.2 %copy-start.3 = (s32[2,1,1,1024,128]{4,3,2,1,0:T(8,128)S(1)}, s32[2,1,1,1024,128]{4,3,2,1,0:T(8,128)}, u32[]{:S(2)}) copy-start(s32[2,1,1,1024,128]{4,3,2,1,0:T(8,128)} %param.8) | copy-start | bytes 3145732
  34.7 4.9 %copy-start.2 = (s32[1,1536]{1,0:T(1,128)S(1)}, s32[1,1536]{1,0:T(1,128)}, u32[]{:S(2)}) copy-start(s32[1,1536]{1,0:T(1,128)} %get-tuple-element.13.order_a) | copy-start | bytes 18436
  37.9 7.5 %collective-permute-start.5 = (bf16[8,128,128]{2,1,0:T(8,128)(2,1)S(1)}, bf16[8,128,128]{2,1,0:T(8,128)(2,1)S(1)}, u32[]{:S(2)}, u32[]{:S(2)}) collective-permute-start(bf16[8,128,128]{2,1,0:T(8,128)(2,1)S(1)} %apply.4.after.refs_0_), channel_id=1, source_target_pairs={{0,2},{1,3},{6,4},{7,5},{8,10},{9,11},{14,12},{15,13},{16,18},{17,... | collective-permute-start | bytes 786440 | tf_op jit(solution)/shard_map/ppermute | solution.py:646
  72.5 11.1 %collective-permute-start.6 = (bf16[8,128,128]{2,1,0:T(8,128)(2,1)S(1)}, bf16[8,128,128]{2,1,0:T(8,128)(2,1)S(1)}, u32[]{:S(2)}, u32[]{:S(2)}) collective-permute-start(bf16[8,128,128]{2,1,0:T(8,128)(2,1)S(1)} %apply.6.after.refs_0_), channel_id=1, source_target_pairs={{0,2},{1,3},{6,4},{7,5},{8,10},{9,11},{14,12},{15,13},{16,18},{17,... | collective-permute-start | bytes 786440 | tf_op jit(solution)/shard_map/ppermute | solution.py:646
